TPU v7x, 32 devices: a whole 2x2x4 slice. The times are simulated.
32 devices in a mesh: groups: 2 (over y), seq: 4 (over z), fsdp: 2 (over x), sub: 2 (over core).
Axes of the slice: x: 2, y: 2, z: 4, core: 2. Of those that a mesh axis runs over, the one named last changes fastest.
Arguments:
- tokens: bfloat16 [2048, 8192], P(('groups', 'seq')), parts along dimension 0, may hold values from -400 to 400
- norm_gain: float32 [8192], replicated, may hold values from 0.1 to 1.9
- w_query: bfloat16 [8, 16, 8192], P(('seq', 'sub'), 'fsdp'), may hold values from -0.0625 to 0.0625
- w_key: bfloat16 [8, 16, 8192], P(('seq', 'sub'), 'fsdp'), may hold values from -0.0625 to 0.0625
- w_value: bfloat16 [8, 128, 8192], P(('seq', 'sub'), 'fsdp'), may hold values from -5 to 5
- head_gain: float32 [128], replicated, may hold values from 0.1 to 1.9
- w_out: bfloat16 [8, 128, 8192], P('seq', None, ('fsdp', 'sub')), may hold values from -0.1875 to 0.1875
Outputs:
- mixed: bfloat16 [2048, 8192], P(('groups', 'seq'), ('fsdp', 'sub')), parts along dimension 0
There are 2 independent parts, one for each index of `groups`. A program takes and returns all parts, laid end to end along the dimension named above; an argument that names none is the same for every part. Nothing has to cross between parts.
All inputs are finite; a program needn't handle non-finite values.
Results may differ from a plain program's by a relative error of at most 0.0084.
Values may be sent and summed in bfloat16 or wider, within the bound.
A program may use at most 64 MiB of HBM per device.

v0:
```python
import math

import jax
import jax.numpy as jnp
import numpy as np
from jax import lax
from jax.sharding import PartitionSpec as P

BLOCK = 512


def taylor_first(vectors):
    feature_count = vectors.shape[0]
    first_row, second_row = np.triu_indices(feature_count, 1)
    cross_terms = vectors[first_row] * vectors[second_row] / 4.0
    squares = vectors * vectors / (4.0 * math.sqrt(2.0))
    leading = jnp.ones((1,) + vectors.shape[1:], jnp.float32)
    return jnp.concatenate([leading, vectors / 2.0, cross_terms, squares], 0)


def head_norm(numerator, head_gain, channel_axis):
    widened = numerator.astype(jnp.float32)
    meansq = jnp.mean(widened * widened, axis=channel_axis, keepdims=True)
    gain_shape = tuple((-1 if axis_pos == channel_axis else 1 for axis_pos in range(widened.ndim)))
    return (widened * lax.rsqrt(meansq + 1e-06) * head_gain.reshape(gain_shape)).astype(
        jnp.bfloat16
    )


def attend(queries, key_vectors, values_local):
    length = queries.shape[1]
    nblocks = length // BLOCK
    channels = values_local.shape[0]
    query_feats = taylor_first(queries.astype(jnp.float32)).astype(jnp.bfloat16)
    key_feats = taylor_first(key_vectors.astype(jnp.float32)).astype(jnp.bfloat16)
    taylor_width = query_feats.shape[0]
    contrib = jnp.einsum(
        "fbj,ebj->bfe",
        key_feats.reshape(taylor_width, nblocks, BLOCK),
        values_local.reshape(channels, nblocks, BLOCK),
        preferred_element_type=jnp.float32,
    )
    prefix = jnp.concatenate([jnp.zeros_like(contrib[:1]), jnp.cumsum(contrib[:-1], axis=0)], 0)
    prior_state = prefix.astype(jnp.bfloat16)
    carried = jnp.einsum(
        "bfe,fbt->bet",
        prior_state,
        query_feats.reshape(taylor_width, nblocks, BLOCK),
        preferred_element_type=jnp.float32,
    )
    earlier = lax.broadcasted_iota(jnp.int32, (BLOCK, BLOCK), 0)
    column_pos = lax.broadcasted_iota(jnp.int32, (BLOCK, BLOCK), 1)
    causal = earlier <= column_pos

    def one_block(block_index):
        offset = block_index * BLOCK
        query_block = lax.dynamic_slice_in_dim(queries, offset, BLOCK, 1)
        key_block = lax.dynamic_slice_in_dim(key_vectors, offset, BLOCK, 1)
        value_block = lax.dynamic_slice_in_dim(values_local, offset, BLOCK, 1)
        scores = jnp.einsum("fj,ft->jt", key_block, query_block, preferred_element_type=jnp.float32)
        kernel = 1.0 + scores / 4.0 + scores * scores / 32.0
        weight = jnp.where(causal, kernel, 0.0).astype(jnp.bfloat16)
        return jnp.einsum("ej,jt->et", value_block, weight, preferred_element_type=jnp.float32)

    local_part = lax.map(one_block, jnp.arange(nblocks, dtype=jnp.int32))
    numerator = (local_part + carried).astype(jnp.bfloat16)
    return jnp.transpose(numerator, (1, 0, 2)).reshape(channels, length)


def per_device(tokens, norm_gain, w_query, w_key, w_value, head_gain, w_out):
    feat_dev = w_query.shape[1]
    inputs = tokens.astype(jnp.float32)
    meansq = jnp.mean(inputs * inputs, axis=1, keepdims=True)
    normed = (inputs * lax.rsqrt(meansq + 1e-05) * norm_gain).astype(jnp.bfloat16)
    stacked = jnp.concatenate([w_query, w_key, w_value], 1)
    head_weights, out_weights = (
        lax.all_gather(stacked, "seq", axis=0, tiled=True),
        lax.all_gather(w_out, "seq", axis=0, tiled=True),
    )
    projected = jnp.einsum(
        "hcd,td->hct", head_weights, normed, preferred_element_type=jnp.float32
    ).astype(jnp.bfloat16)
    by_head = lax.all_to_all(projected, "seq", split_axis=0, concat_axis=2, tiled=True)
    qk_local = by_head[:, : 2 * feat_dev]
    values_local = by_head[0, 2 * feat_dev :]
    qk_whole = lax.all_gather(qk_local, "fsdp", axis=0, tiled=True)
    length = qk_whole.shape[2]
    queries = qk_whole[:, :feat_dev].reshape(-1, length)
    key_vectors = qk_whole[:, feat_dev:].reshape(-1, length)
    numerator = attend(queries, key_vectors, values_local)
    heads_total = out_weights.shape[0]
    head_width = out_weights.shape[1]
    by_token = lax.all_to_all(numerator[None], "seq", split_axis=2, concat_axis=0, tiled=True)
    everyone = lax.all_gather(by_token[None], ("fsdp", "sub"), axis=0, tiled=True)
    arranged = everyone.reshape(
        lax.axis_size("fsdp"),
        lax.axis_size("sub"),
        everyone.shape[1],
        everyone.shape[2],
        everyone.shape[3],
    )
    arranged = jnp.transpose(arranged, (2, 1, 0, 3, 4)).reshape(heads_total, head_width, -1)
    attended = head_norm(arranged, head_gain, 1)
    mixed = jnp.einsum("het,hed->td", attended, out_weights, preferred_element_type=jnp.float32)
    return mixed.astype(jnp.bfloat16)


def solution(mesh):
    in_specs = (
        P(("groups", "seq"), None),
        P(),
        P(("seq", "sub"), "fsdp", None),
        P(("seq", "sub"), "fsdp", None),
        P(("seq", "sub"), "fsdp", None),
        P(),
        P("seq", None, ("fsdp", "sub")),
    )
    out_specs = P(("groups", "seq"), ("fsdp", "sub"))
    return jax.shard_map(
        per_device, mesh=mesh, in_specs=in_specs, out_specs=out_specs, check_vma=False
    )
```

profile of v0, /device:TPU:0, one launch (start us, length us, event | category | flops | bytes accessed | tf_op | source)
XLA Modules:
  0.0 208.2 jit_solution(16304550115294808762)
XLA Ops:
  6.5 2.5 %pad_maximum_fusion = bf16[1,80,8192]{2,1,0:T(8,128)(2,1)} fusion(bf16[1,64,8192]{2,1,0:T(8,128)(2,1)} %param.21, bf16[1,8,8192]{2,1,0:T(8,128)(2,1)} %param.20, bf16[1,8,8192]{2,1,0:T(8,128)(2,1)} %param.19), kind=kLoop, calls=%fused_computation.32 | loop fusion | flops 3932160 | bytes 2621440 | tf_op jit(solution)/shard_map/concatenate | solution.py:75
  9.1 0.7 all-gather.6.cloned.1.call-update
  9.8 3.1 %fusion.18 = f32[256]{0:T(256)S(1)} fusion(bf16[256,8192]{1,0:T(8,128)(2,1)} %param.17), kind=kLoop, calls=%fused_computation.23 | loop fusion | flops 6291200 | bytes 4195328 | tf_op jit(solution)/shard_map/reduce_sum | solution.py:73
  12.9 97.0 %all-gather.4.cloned.1.call-done = bf16[4,80,8192]{2,1,0:T(8,128)(2,1)} async-done(((bf16[1,80,8192]{2,1,0:T(8,128)(2,1)}), bf16[4,80,8192]{2,1,0:T(8,128)(2,1)}) %all-gather.4.cloned.1.call-update) | async-done | bytes 5242896 | tf_op jit(solution)/shard_map/all_gather | solution.py:77
  110.0 6.1 %fusion.27 = bf16[4,80,256]{2,1,0:T(8,128)(2,1)} fusion(bf16[4,80,8192]{2,1,0:T(8,128)(2,1)} %all-gather.4.cloned.1.call-done, bf16[256,8192]{1,0:T(8,128)(2,1)} %param.17, f32[8192]{0:T(1024)S(1)} %copy-done.2, f32[256]{0:T(256)S(1)} %add_rsqrt_fusion), kind=kOutput, calls=%fused_computation.34 | convolution fusion | flops 1350647808 | bytes 9634816 | tf_op jit(solution)/shard_map/hcd,td->hct/dot_general | solution.py:80
  116.0 3.3 %all-to-all-start = ((bf16[4,80,256]{2,1,0:T(8,128)(2,1)}), bf16[4,80,256]{2,1,0:T(8,128)(2,1)S(1)}, u32[]{:S(2)}, u32[]{:S(2)}) async-start(bf16[4,80,256]{2,1,0:T(8,128)(2,1)} %fusion.27), calls=%async_computation | async-start | bytes 327680 | tf_op jit(solution)/shard_map/all_to_all | solution.py:83
  119.5 11.4 %all-to-all-done = bf16[4,80,256]{2,1,0:T(8,128)(2,1)S(1)} async-done(((bf16[4,80,256]{2,1,0:T(8,128)(2,1)}), bf16[4,80,256]{2,1,0:T(8,128)(2,1)S(1)}, u32[]{:S(2)}, u32[]{:S(2)}) %all-to-all-start) | async-done | bytes 163872 | tf_op jit(solution)/shard_map/all_to_all | solution.py:83
  130.9 4.6 %all_gather.13 = bf16[2,16,1024]{2,1,0:T(8,128)(2,1)S(1)} all-gather(bf16[1,16,1024]{2,1,0:T(8,128)(2,1)S(1)} %slice.30), channel_id=1, replica_groups=mesh['groups'=2,'seq'=4,'fsdp'=2,'sub'=2] {'fsdp'}, dimensions={0}, use_global_device_ids=true | all-gather | bytes 98304 | tf_op jit(solution)/shard_map/all_gather | solution.py:86
  135.5 0.8 gather_fusion
  136.3 0.8 gather_fusion.1
  137.1 0.8 gather_fusion.2
  137.9 0.8 gather_fusion.3
  139.5 3.5 %while.11 = (s32[]{:T(128)}, f32[2,64,512]{2,1,0:T(8,128)S(1)}, s32[2]{0:T(128)S(1)}, bf16[64,1024]{1,0:T(8,128)(2,1)S(1)}, bf16[16,1024]{1,0:T(8,128)(2,1)S(1)}...) while((s32[]{:T(128)}, f32[2,64,512]{2,1,0:T(8,128)S(1)}, ...), condition=%wide.region_2.3_spmd.clone, body=%wide.region_1.0_spmd.clone.sunk | while | flops 44040196 | bytes 231075 | solution.py:65
  139.5 0.6 dynamic_slice.32
  140.7 0.5 fusion.70
  141.2 0.6 dynamic_slice.32
  142.5 0.5 fusion.70
  143.6 0.5 broadcast.135
  144.1 2.3 %reduce.7 = bf16[1024,64]{1,0:T(8,128)(2,1)S(1)} reduce(bf16[1024,1,64]{2,1,0:T(2,128)(2,1)S(1)} %bitcast.63, bf16[]{:T(256)} %broadcast.135), dimensions={1}, to_apply=%bitcast.51.reduce_sub_computation | reduce | bytes 262146
  146.6 13.8 %all_to_all.33 = bf16[4,2,8192]{2,1,0:T(2,128)(2,1)S(1)} all-to-all(bf16[4,2,8192]{2,1,0:T(2,128)(2,1)S(1)} %reshape.137), channel_id=1, replica_groups=mesh['groups'=2,'seq'=4,'fsdp'=2,'sub'=2] {'seq'}, dimensions={0} | all-to-all | bytes 262144 | tf_op jit(solution)/shard_map/all_to_all | solution.py:93
  160.8 0.3 copy.76
  161.2 7.1 %all-gather = bf16[16,1,64,256]{3,2,1,0:T(8,128)(2,1)S(1)} all-gather(bf16[4,1,64,256]{3,2,1,0:T(8,128)(2,1)S(1)} %copy.77), channel_id=2, replica_groups=mesh['groups'=2,'seq'=4,'fsdp'=2,'sub'=2] {'fsdp','sub'}, dimensions={0}, use_global_device_ids=true | all-gather | bytes 655360 | tf_op jit(solution)/shard_map/all_gather | solution.py:94
  168.8 28.0 %all-gather.6.cloned.1.call-done = bf16[8,128,2048]{2,1,0:T(8,128)(2,1)} async-done(((bf16[2,128,2048]{2,1,0:T(8,128)(2,1)}), bf16[8,128,2048]{2,1,0:T(8,128)(2,1)}) %all-gather.6.cloned.1.call-update) | async-done | bytes 4194320 | tf_op jit(solution)/shard_map/all_gather | solution.py:78
  196.8 4.5 %fusion.26 = bf16[256,2048]{1,0:T(8,128)(2,1)} fusion(bf16[8,128,2048]{2,1,0:T(8,128)(2,1)} %all-gather.6.cloned.1.call-done, f32[8,128,256]{2,1,0:T(8,128)S(1)} %bitcast.64, f32[128]{0:T(128)S(1)} %copy-done.3, f32[8,256]{1,0:T(8,128)S(1)} %rsqrt.21), kind=kOutput, calls=%fused_computation.31 | convolution fusion | flops 1075052544 | bytes 6300160 | tf_op jit(solution)/shard_map/het,hed->td/dot_general | solution.py:104
  (51 shorter events, 2.4 us)
Async XLA Ops:
  6.5 103.4 %copy-start.2 = (f32[8192]{0:T(1024)S(1)}, f32[8192]{0:T(1024)}, u32[]{:S(2)}) copy-start(f32[8192]{0:T(1024)} %param.18) | copy-start | bytes 98308
  6.5 103.4 %all-gather.4.cloned.1.call-start = ((), (), s32[]{:S(2)}) async-start(), calls=%async_computation.2 | async-start | bytes 6553600 | tf_op jit(solution)/shard_map/all_gather | solution.py:77
  9.0 187.8 %all-gather.6.cloned.1.call-start = ((), (), s32[]{:S(2)}) async-start(), calls=%async_computation.3 | async-start | bytes 5242880 | tf_op jit(solution)/shard_map/all_gather | solution.py:78
  12.9 106.5 %copy-start.1 = (s32[120]{0:T(128)S(1)}, s32[120]{0:T(128)}, u32[]{:S(2)}) copy-start(s32[120]{0:T(128)} %constant.78) | copy-start | bytes 1444
  12.9 106.5 %copy-start = (s32[120]{0:T(128)S(1)}, s32[120]{0:T(128)}, u32[]{:S(2)}) copy-start(s32[120]{0:T(128)} %constant.79) | copy-start | bytes 1444
  116.0 14.8 %all-to-all-start = ((bf16[4,80,256]{2,1,0:T(8,128)(2,1)}), bf16[4,80,256]{2,1,0:T(8,128)(2,1)S(1)}, u32[]{:S(2)}, u32[]{:S(2)}) async-start(bf16[4,80,256]{2,1,0:T(8,128)(2,1)} %fusion.27), calls=%async_computation | async-start | bytes 327680 | tf_op jit(solution)/shard_map/all_to_all | solution.py:83
  143.6 53.3 %copy-start.3 = (f32[128]{0:T(128)S(1)}, f32[128]{0:T(128)}, u32[]{:S(2)}) copy-start(f32[128]{0:T(128)} %param.22) | copy-start | bytes 1540
Sparse Core Ops, SparseCore 0:
  9.2 100.7 all-gather.3
  111.5 85.2 all-gather.5
where the time goes:
time: 209 us; the launch traced here: 208 us
  waiting for transfers between devices  137 us (66%)
  blocking collectives  25.6 us (12%)
  between operations  13.8 us (7%)
  matrix products  12.1 us (6%)
  other arithmetic  8.29 us (4%)
  local copies, waits for them, and re-layouts  6.51 us (3%)
  starting transfers between devices  3.39 us (2%)
    all_gather x1, waiting for transfers between devices, per_device(): lax.all_gather(stacked, 'seq', axis=0, tiled=True)  97 us
    all_gather x1, waiting for transfers between devices, per_device(): lax.all_gather(w_out, 'seq', axis=0, tiled=True)  28 us
    all_to_all x1, blocking collectives, per_device(): lax.all_to_all(numerator[None], 'seq', split_axis=2, concat_axis=0, tiled...  13.8 us
    all_to_all x1, waiting for transfers between devices, per_device(): lax.all_to_all(projected, 'seq', split_axis=0, concat_axis=2, tiled=True)  11.4 us
    all_gather x1, blocking collectives, per_device(): lax.all_gather(by_token[None], ('fsdp', 'sub'), axis=0, tiled=True)  7.15 us
    dot_general x1, matrix products, per_device(): jnp.einsum('hcd,td->hct', head_weights, normed, preferred_element_type=jn...  6.07 us
    all_gather x1, blocking collectives, per_device(): qk_whole = lax.all_gather(qk_local, 'fsdp', axis=0, tiled=True)  4.58 us
    dot_general x1, matrix products, per_device(): jnp.einsum('het,hed->td', attended, out_weights, preferred_element_type=j...  4.52 us
  transfers between devices with their start and end apart: 3, of which 3 were waited for; matrix products, arithmetic and copies ran while one was open for 10% of the time, Pallas kernels for 0%

commit v1 on v0

v1 whole, which is shorter than its diff:
```python
import functools

import jax
import jax.numpy as jnp
from jax import lax
from jax.experimental import pallas as pl
from jax.experimental.pallas import tpu as pltpu
from jax.sharding import PartitionSpec as P

MESH = pl.DeviceIdType.MESH
F32 = jnp.float32
BF16 = jnp.bfloat16


def kernel(
    n,
    nf,
    ns,
    pieces,
    out_pieces,
    tok_ref,
    gain_ref,
    w_ref,
    head_gain_ref,
    wo_ref,
    out_ref,
    normed,
    wbuf,
    wobuf,
    qk_send,
    v_send,
    qk_all,
    v_all,
    q_full,
    k_full,
    num_send,
    num_all,
    attended,
    total,
    w_zrecv,
    w_yrecv,
    w_right,
    w_left,
    w_across,
    o_zrecv,
    o_yrecv,
    o_right,
    o_left,
    o_across,
    qk_ssem,
    qk_rsem,
    v_ssem,
    v_rsem,
    num_ssem,
    num_rsem,
    sib_ssem,
    sib_rsem,
):
    group = lax.axis_index("groups")
    me = lax.axis_index("seq")
    my_f = lax.axis_index("fsdp")
    my_s = lax.axis_index("sub")
    tokens, width = tok_ref.shape
    span = width // (2 * pieces)
    qk_rows = qk_all.shape[2]
    half_rows = qk_rows // 2

    def own_w(c):
        start = pl.multiple_of((group * pieces + c) * span, span)
        return w_ref.at[:, pl.ds(start, span)]

    def own_o(c):
        return wo_ref.at[group, c]

    class Stream:
        def __init__(self, own, buf, count, zrecv, yrecv, right, left, across):
            self.own, self.buf, self.count = own, buf, count
            self.zrecv, self.yrecv = zrecv, yrecv
            self.right_sem, self.left_sem, self.across_sem = right, left, across

        def along(self, o, c, sems, target, own):
            slot = self.buf.at[o, group, c]
            return pltpu.make_async_remote_copy(
                src_ref=self.own(c) if own else slot,
                dst_ref=slot,
                send_sem=sems.at[o, c],
                recv_sem=self.zrecv.at[o, c],
                device_id={"seq": target},
                device_id_type=MESH,
            )

        def right(self, o, c, own=False):
            return self.along(o, c, self.right_sem, me + 1, own)

        def left(self, o, c, own=False):
            return self.along(o, c, self.left_sem, me - 1, own)

        def across(self, o, c, half):
            slot = self.buf.at[o, half, c]
            return pltpu.make_async_remote_copy(
                src_ref=slot,
                dst_ref=slot,
                send_sem=self.across_sem.at[o, c],
                recv_sem=self.yrecv.at[o, c],
                device_id={"groups": 1 - group},
                device_id_type=MESH,
            )

        def begin(self):
            for c in range(self.count):

                @pl.when(me + 1 < n)
                def _():
                    self.right(me, c, True).start()

                @pl.when(me >= 1)
                def _():
                    self.left(me, c, True).start()

        def relay(self, r):
            for c in range(self.count):

                @pl.when(me >= r)
                def _():
                    o = me - r
                    self.right(o, c).wait_recv()

                    @pl.when(me + 1 < n)
                    def _():
                        self.right(o, c).start()

                    self.across(o, c, group).start()

                @pl.when(me + r < n)
                def _():
                    o = me + r
                    self.left(o, c).wait_recv()

                    @pl.when(me >= 1)
                    def _():
                        self.left(o, c).start()

                    self.across(o, c, group).start()

        def arrive(self, o):
            for c in range(self.count):
                self.across(o, c, 1 - group).wait_recv()

        def finish(self):
            for r in range(n):
                for c in range(self.count):

                    @pl.when((me >= r) & (me + 1 < n))
                    def _():
                        self.right(me - r, c, r == 0).wait_send()

                    @pl.when((me + r < n) & (me >= 1))
                    def _():
                        self.left(me + r, c, r == 0).wait_send()

                    if r > 0:

                        @pl.when(me >= r)
                        def _():
                            self.across(me - r, c, group).wait_send()

                        @pl.when(me + r < n)
                        def _():
                            self.across(me + r, c, group).wait_send()

    w_stream = Stream(own_w, wbuf, pieces, w_zrecv, w_yrecv, w_right, w_left, w_across)
    o_stream = Stream(own_o, wobuf, out_pieces, o_zrecv, o_yrecv, o_right, o_left, o_across)

    w_stream.begin()

    row_step = 16

    def norm_rows(i, carry):
        rows = pl.ds(pl.multiple_of(i * row_step, row_step), row_step)
        sumsq = jnp.zeros((row_step, 1), F32)
        for c in range(2 * pieces):
            part = tok_ref[rows, c * span : (c + 1) * span].astype(F32)
            sumsq = sumsq + jnp.sum(part * part, axis=1, keepdims=True)
        scale = lax.rsqrt(sumsq / width + 1e-05)
        for c in range(2 * pieces):
            cols = slice(c * span, (c + 1) * span)
            part = tok_ref[rows, cols].astype(F32)
            normed[c, rows, :] = (part * scale * gain_ref[:, cols]).astype(BF16)
        return carry

    lax.fori_loop(0, tokens // row_step, norm_rows, 0)

    def contract(weights, acts):
        return lax.dot_general(weights, acts, (((1,), (1,)), ((), ())), preferred_element_type=F32)

    def qk_copy(o, source, other_f, token_block, f_from):
        return pltpu.make_async_remote_copy(
            src_ref=source,
            dst_ref=qk_all.at[token_block, f_from],
            send_sem=qk_ssem.at[o, other_f],
            recv_sem=qk_rsem.at[token_block, f_from],
            device_id={"seq": o, "fsdp": other_f},
            device_id_type=MESH,
        )

    def v_copy(o, token_block):
        return pltpu.make_async_remote_copy(
            src_ref=v_send.at[o],
            dst_ref=v_all.at[token_block],
            send_sem=v_ssem.at[o],
            recv_sem=v_rsem.at[token_block],
            device_id={"seq": o},
            device_id_type=MESH,
        )

    def project_own():
        acc = jnp.zeros((w_ref.shape[0], tokens), F32)
        for c in range(2 * pieces):
            acc = acc + contract(w_ref[:, c * span : (c + 1) * span], normed[c])
        qk_all[me, my_f] = acc[:qk_rows].astype(BF16)
        v_all[me] = acc[qk_rows:].astype(BF16)
        for df in range(1, nf):
            other = lax.rem(my_f + df, nf)
            qk_copy(me, qk_all.at[me, my_f], other, me, my_f).start()

    def project(o):
        def body(c, acc):
            return acc + contract(wbuf[o, c // pieces, c % pieces], normed[c])

        acc = lax.fori_loop(0, 2 * pieces, body, jnp.zeros((w_ref.shape[0], tokens), F32))
        qk_send[o] = acc[:qk_rows].astype(BF16)
        v_send[o] = acc[qk_rows:].astype(BF16)
        for df in range(nf):
            qk_copy(o, qk_send.at[o], lax.rem(my_f + df, nf), me, my_f).start()
        v_copy(o, me).start()

    def both(r, action):
        @pl.when(me >= r)
        def _():
            action(me - r)

        @pl.when(me + r < n)
        def _():
            action(me + r)

    def take(o):
        w_stream.arrive(o)
        project(o)

    project_own()
    for r in range(1, n):
        w_stream.relay(r)
        if r > 1:
            both(r - 1, take)
    o_stream.begin()
    both(n - 1, take)

    o_stream.relay(1)

    for d in range(1, n):
        t = lax.rem(me + d, n)
        v_copy(me, t).wait_recv()
        for df in range(nf):
            qk_copy(me, qk_all.at[t, df], 0, t, df).wait_recv()
    for df in range(1, nf):
        other = lax.rem(my_f + df, nf)
        qk_copy(me, qk_all.at[me, other], other, me, other).wait_recv()

    for t in range(n):
        parts = [qk_all[t, f].astype(F32) for f in range(nf)]
        q_full[t] = jnp.concatenate([p[:half_rows] for p in parts], 0).astype(BF16)
        k_full[t] = jnp.concatenate([p[half_rows:] for p in parts], 0).astype(BF16)

    channels = v_all.shape[1]
    key_pos = lax.broadcasted_iota(jnp.int32, (tokens, tokens), 0)
    query_pos = lax.broadcasted_iota(jnp.int32, (tokens, tokens), 1)

    def numerator(t):
        queries = q_full[t]

        def body(j, acc):
            scores = lax.dot_general(
                k_full[j], queries, (((0,), (0,)), ((), ())), preferred_element_type=F32
            )
            value = 1.0 + scores * 0.25 + scores * scores * 0.03125
            weight = jnp.where(key_pos + (j - t) * tokens <= query_pos, value, 0.0).astype(BF16)
            return acc + jnp.dot(v_all[j], weight, preferred_element_type=F32)

        acc = lax.fori_loop(0, t + 1, body, jnp.zeros((channels, tokens), F32))
        return acc.astype(BF16)

    def num_copy(t, head_block):
        return pltpu.make_async_remote_copy(
            src_ref=num_send.at[t],
            dst_ref=num_all.at[head_block, my_f, my_s],
            send_sem=num_ssem.at[t],
            recv_sem=num_rsem.at[head_block],
            device_id={"seq": t},
            device_id_type=MESH,
        )

    def sib_copy(o, to_f, to_s, from_f, from_s):
        slot = num_all.at[o, from_f, from_s]
        return pltpu.make_async_remote_copy(
            src_ref=slot,
            dst_ref=slot,
            send_sem=sib_ssem.at[o, to_f, to_s],
            recv_sem=sib_rsem.at[o, from_f, from_s],
            device_id={"fsdp": to_f, "sub": to_s},
            device_id_type=MESH,
        )

    def siblings():
        for df in range(nf):
            for ds in range(ns):
                if df or ds:
                    yield lax.rem(my_f + df, nf), lax.rem(my_s + ds, ns)

    for d in range(1, n):
        t = lax.rem(me + d, n)
        num_send[t] = numerator(t)
        num_copy(t, me).start()
    num_all[me, my_f, my_s] = numerator(me)
    for f, s in siblings():
        sib_copy(me, f, s, my_f, my_s).start()

    for r in range(2, n):
        o_stream.relay(r)
        if r == 2:
            for d in range(1, n):
                o = lax.rem(me + d, n)
                num_copy(o, o).wait_recv()
                for f, s in siblings():
                    sib_copy(o, f, s, my_f, my_s).start()

    for d in range(n):
        o = lax.rem(me + d, n)
        for f, s in siblings():
            sib_copy(o, f, s, f, s).wait_recv()

    head_width = nf * channels

    def attend_block(o, carry):
        for s in range(ns):
            whole = jnp.concatenate([num_all[o, f, s] for f in range(nf)], 0).astype(F32)
            meansq = jnp.sum(whole * whole, axis=0, keepdims=True) / head_width
            scaled = whole * lax.rsqrt(meansq + 1e-06) * head_gain_ref[...]
            attended[o, :, s * head_width : (s + 1) * head_width] = scaled.T.astype(BF16)
        return carry

    lax.fori_loop(0, n, attend_block, 0)

    columns = out_ref.shape[1]
    depth = ns * head_width

    total[...] = jnp.dot(
        attended[me], wo_ref[...].reshape(depth, columns), preferred_element_type=F32
    )

    def multiply(o):
        o_stream.arrive(o)
        total[...] += jnp.dot(
            attended[o], wobuf[o].reshape(depth, columns), preferred_element_type=F32
        )

    for r in range(1, n):
        both(r, multiply)
    out_ref[...] = total[...].astype(BF16)

    w_stream.finish()
    o_stream.finish()
    for d in range(n):
        o = lax.rem(me + d, n)
        for df in range(nf):
            if d or df:
                other = lax.rem(my_f + df, nf)
                source = qk_send.at[o] if d else qk_all.at[me, my_f]
                qk_copy(o, source, other, me, my_f).wait_send()
        if d:
            v_copy(o, me).wait_send()
            num_copy(o, me).wait_send()
        for f, s in siblings():
            sib_copy(o, f, s, my_f, my_s).wait_send()


def per_device(sizes, tokens, norm_gain, w_query, w_key, w_value, head_gain, w_out):
    n, nf, ns = sizes
    stacked = jnp.concatenate([w_query[0], w_key[0], w_value[0]], 0)
    rows, width = stacked.shape
    count = tokens.shape[0]
    qk_rows = w_query.shape[1] + w_key.shape[1]
    channels = w_value.shape[1]
    head_width, columns = w_out.shape[1], w_out.shape[2]
    pieces = max(1, 16 // n)
    out_pieces = max(1, 16 // n)
    wo = w_out.reshape(ns, out_pieces, head_width // out_pieces, columns)
    vmem = pl.BlockSpec(memory_space=pltpu.VMEM)
    dma = pltpu.SemaphoreType.DMA
    return pl.pallas_call(
        functools.partial(kernel, n, nf, ns, pieces, out_pieces),
        out_shape=jax.ShapeDtypeStruct((count, columns), BF16),
        in_specs=[vmem] * 5,
        out_specs=vmem,
        scratch_shapes=[
            pltpu.VMEM((2 * pieces, count, width // (2 * pieces)), BF16),
            pltpu.VMEM((n, 2, pieces, rows, width // (2 * pieces)), BF16),
            pltpu.VMEM((n,) + wo.shape, BF16),
            pltpu.VMEM((n, qk_rows, count), BF16),
            pltpu.VMEM((n, channels, count), BF16),
            pltpu.VMEM((n, nf, qk_rows, count), BF16),
            pltpu.VMEM((n, channels, count), BF16),
            pltpu.VMEM((n, nf * qk_rows // 2, count), BF16),
            pltpu.VMEM((n, nf * qk_rows // 2, count), BF16),
            pltpu.VMEM((n, channels, count), BF16),
            pltpu.VMEM((n, nf, ns, channels, count), BF16),
            pltpu.VMEM((n, count, ns * head_width), BF16),
            pltpu.VMEM((count, columns), F32),
        ]
        + [dma((n, pieces))] * 5
        + [dma((n, out_pieces))] * 5
        + [
            dma((n, nf)),
            dma((n, nf)),
            dma((n,)),
            dma((n,)),
            dma((n,)),
            dma((n,)),
            dma((n, nf, ns)),
            dma((n, nf, ns)),
        ],
        compiler_params=pltpu.CompilerParams(
            has_side_effects=True, vmem_limit_bytes=60 * 1024 * 1024
        ),
    )(tokens, norm_gain.reshape(1, -1), stacked, head_gain.reshape(-1, 1), wo)


def solution(mesh):
    in_specs = (
        P(("groups", "seq"), None),
        P(),
        P(("seq", "sub"), "fsdp", None),
        P(("seq", "sub"), "fsdp", None),
        P(("seq", "sub"), "fsdp", None),
        P(),
        P("seq", None, ("fsdp", "sub")),
    )
    out_specs = P(("groups", "seq"), ("fsdp", "sub"))
    sizes = (mesh.shape["seq"], mesh.shape["fsdp"], mesh.shape["sub"])
    return jax.shard_map(
        functools.partial(per_device, sizes),
        mesh=mesh,
        in_specs=in_specs,
        out_specs=out_specs,
        check_vma=False,
    )
```

time: 209 us -> 116 us (0.56)
  waiting for transfers between devices: 137 us -> 0 us
  Pallas kernels: 0 us -> 109 us
  blocking collectives: 25.6 us -> 0 us
  between operations: 13.8 us -> 0.01 us
  matrix products: 12.1 us -> 0 us
  other arithmetic: 8.29 us -> 2.45 us
  starting transfers between devices: 3.39 us -> 0 us
  local copies, waits for them, and re-layouts: 6.51 us -> 3.69 us
    all_gather x2 -> x0, waiting for transfers between devices: 125 us -> none  [the longest x1 97 us: per_device(): lax.all_gather(stacked, 'seq', axis=0, tiled=True)]
    pallas_call x0 -> x1, Pallas kernels: none -> 109 us  [per_device(): pl.pallas_call(functools.partial(kernel, n, nf, ns, pieces, out_pieces),...]
    all_to_all x1 -> x0, blocking collectives: 13.8 us -> none  [per_device(): lax.all_to_all(numerator[None], 'seq', split_axis=2, concat_axis=0, tiled...]
    dot_general x6 -> x0, matrix products: 12.1 us -> none  [the longest x1 6.07 us: per_device(): jnp.einsum('hcd,td->hct', head_weights, normed, preferred_element_type=jn...]
    all_gather x2 -> x0, blocking collectives: 11.7 us -> none  [the longest x1 7.15 us: per_device(): lax.all_gather(by_token[None], ('fsdp', 'sub'), axis=0, tiled=True)]
    all_to_all x1 -> x0, waiting for transfers between devices: 11.4 us -> none  [per_device(): lax.all_to_all(projected, 'seq', split_axis=0, concat_axis=2, tiled=True)]
    all_to_all x1 -> x0, starting transfers between devices: 3.35 us -> none  [per_device(): lax.all_to_all(projected, 'seq', split_axis=0, concat_axis=2, tiled=True)]
    reduce_sum x3 -> x0, other arithmetic: 3.25 us -> none  [the longest x1 3.1 us: per_device(): meansq = jnp.mean(inputs * inputs, axis=1, keepdims=True)]
  transfers between devices with their start and end apart: 3 -> 0, of which waited for: 3 -> 0; matrix products, arithmetic and copies ran while one was open for 10% -> 0% of each run, Pallas kernels for 0% -> 0%
where the time goes in v1:
time: 116 us; the launch traced here: 115 us
  Pallas kernels  109 us (94%)
  local copies, waits for them, and re-layouts  3.69 us (3%)
  other arithmetic  2.45 us (2%)
    pallas_call x1, Pallas kernels, per_device(): pl.pallas_call(functools.partial(kernel, n, nf, ns, pieces, out_pieces),...  109 us
    concatenate x1, other arithmetic, per_device(): stacked = jnp.concatenate([w_query[0], w_key[0], w_value[0]], 0)  2.45 us

profile of v1, /device:TPU:0, one launch (start us, length us, event | category | flops | bytes accessed | tf_op | source)
XLA Modules:
  0.0 115.5 jit_solution(7161129027917796469)
XLA Ops:
  0.0 1.4 %copy.8.head_gain_ref = f32[128,1]{1,0:T(8,128)} copy(f32[128,1]{0,1:T(1,128)} %bitcast.11) | data formatting | bytes 1024 | tf_op jit(solution)/shard_map/reshape | solution.py:434
  1.4 2.5 %pad_maximum_fusion.w_ref = bf16[80,8192]{1,0:T(8,128)(2,1)} fusion(bf16[64,8192]{1,0:T(8,128)(2,1)} %bitcast.6, bf16[8,8192]{1,0:T(8,128)(2,1)} %bitcast.8, bf16[8,8192]{1,0:T(8,128)(2,1)} %bitcast.9), kind=kLoop, calls=%fused_computation | loop fusion | flops 3932160 | bytes 2621440 | tf_op jit(solution)/shard_map/concatenate | solution.py:388
  3.8 109.3 %shard_map.73 = bf16[256,2048]{1,0:T(8,128)(2,1)} custom-call(bf16[256,8192]{1,0:T(8,128)(2,1)} %tok_ref.1, f32[1,8192]{1,0:T(1,128)} %bitcast.10, bf16[80,8192]{1,0:T(8,128)(2,1)} %pad_maximum_fusion.w_ref, f32[128,1]{1,0:T(8,128)} %copy.8.head_gain_ref, bf16[2,4,32,2048]{3,2,1,0:T(8,128)(2,1)} %bitcast.7), custom_call_target="tpu_custom_call" | custom-call | tf_op jit(solution)/shard_map/pallas_call | solution.py:399
  113.2 2.3 %copy.10 = bf16[256,2048]{1,0:T(8,128)(2,1)} copy(bf16[256,2048]{1,0:T(8,128)(2,1)} %shard_map.73) | data formatting | bytes 2097152

commit v2 on v1

--- a/solution.py
+++ b/solution.py
@@ -18,12 +18,35 @@
     ns,
     pieces,
     out_pieces,
+    w_count,
+    tok_hbm,
+    gain_ref,
+    head_gain_ref,
+    wo_hbm,
+    *rest,
+):
+    kernel_body(
+        n, nf, ns, pieces, out_pieces, tok_hbm, gain_ref, head_gain_ref, wo_hbm,
+        rest[:w_count], *rest[w_count:]
+    )
+
+
+def kernel_body(
+    n,
+    nf,
+    ns,
+    pieces,
+    out_pieces,
+    tok_hbm,
+    gain_ref,
+    head_gain_ref,
+    wo_hbm,
+    w_hbm,
+    out_ref,
     tok_ref,
-    gain_ref,
     w_ref,
-    head_gain_ref,
     wo_ref,
-    out_ref,
+    load_sem,
     normed,
     wbuf,
     wobuf,
@@ -61,6 +84,37 @@
     my_f = lax.axis_index("fsdp")
     my_s = lax.axis_index("sub")
     tokens, width = tok_ref.shape
+
+    loads = []
+    row = 0
+    for k, source in enumerate(w_hbm):
+        size = source.shape[0]
+        target = w_ref.at[pl.ds(row, size)] if len(w_hbm) > 1 else w_ref
+        loads.append(pltpu.make_async_copy(source, target, load_sem.at[k]))
+        row += size
+    tok_load = pltpu.make_async_copy(tok_hbm, tok_ref, load_sem.at[len(w_hbm)])
+    wo_load = pltpu.make_async_copy(wo_hbm, wo_ref, load_sem.at[len(w_hbm) + 1])
+    for load in loads + [tok_load, wo_load]:
+        load.start()
+
+    peers = [
+        {"seq": lax.rem(me + dz, n), "fsdp": lax.rem(my_f + df, nf)}
+        for dz in range(n)
+        for df in range(nf)
+        if dz or df
+    ]
+    peers += [
+        {"fsdp": lax.rem(my_f + df, nf), "sub": lax.rem(my_s + ds, ns)}
+        for df in range(nf)
+        for ds in range(1, ns)
+    ]
+    peers += [{"groups": 1 - group}]
+    barrier = pltpu.get_barrier_semaphore()
+    for peer in peers:
+        pl.semaphore_signal(barrier, inc=1, device_id=peer, device_id_type=MESH)
+    pl.semaphore_wait(barrier, len(peers))
+    for load in loads:
+        load.wait()
     span = width // (2 * pieces)
     qk_rows = qk_all.shape[2]
     half_rows = qk_rows // 2
@@ -117,8 +171,10 @@
                 def _():
                     self.left(me, c, True).start()
 
-        def relay(self, r):
+        def relay(self, r, between=None):
             for c in range(self.count):
+                if between is not None and c == self.count // 2:
+                    between()
 
                 @pl.when(me >= r)
                 def _():
@@ -172,6 +228,14 @@
     o_stream = Stream(own_o, wobuf, out_pieces, o_zrecv, o_yrecv, o_right, o_left, o_across)
 
     w_stream.begin()
+    wo_load.wait()
+    at_end = (me == 0) | (me == n - 1)
+
+    @pl.when(at_end)
+    def _():
+        o_stream.begin()
+
+    tok_load.wait()
 
     row_step = 16
 
@@ -249,27 +313,30 @@
 
     project_own()
     for r in range(1, n):
-        w_stream.relay(r)
-        if r > 1:
-            both(r - 1, take)
-    o_stream.begin()
-    both(n - 1, take)
-
-    o_stream.relay(1)
-
-    for d in range(1, n):
-        t = lax.rem(me + d, n)
-        v_copy(me, t).wait_recv()
-        for df in range(nf):
-            qk_copy(me, qk_all.at[t, df], 0, t, df).wait_recv()
-    for df in range(1, nf):
-        other = lax.rem(my_f + df, nf)
-        qk_copy(me, qk_all.at[me, other], other, me, other).wait_recv()
-
-    for t in range(n):
-        parts = [qk_all[t, f].astype(F32) for f in range(nf)]
-        q_full[t] = jnp.concatenate([p[:half_rows] for p in parts], 0).astype(BF16)
-        k_full[t] = jnp.concatenate([p[half_rows:] for p in parts], 0).astype(BF16)
+        if r == n - 1:
+
+            @pl.when(jnp.logical_not(at_end))
+            def _():
+                o_stream.begin()
+
+        w_stream.relay(r, functools.partial(both, r - 1, take) if r > 1 else None)
+
+    o_stream.relay(1, functools.partial(both, n - 1, take))
+
+    def gather_heads():
+        for d in range(1, n):
+            t = lax.rem(me + d, n)
+            v_copy(me, t).wait_recv()
+            for df in range(nf):
+                qk_copy(me, qk_all.at[t, df], 0, t, df).wait_recv()
+        for df in range(1, nf):
+            other = lax.rem(my_f + df, nf)
+            qk_copy(me, qk_all.at[me, other], other, me, other).wait_recv()
+
+        for t in range(n):
+            parts = [qk_all[t, f].astype(F32) for f in range(nf)]
+            q_full[t] = jnp.concatenate([p[:half_rows] for p in parts], 0).astype(BF16)
+            k_full[t] = jnp.concatenate([p[half_rows:] for p in parts], 0).astype(BF16)
 
     channels = v_all.shape[1]
     key_pos = lax.broadcasted_iota(jnp.int32, (tokens, tokens), 0)
@@ -316,22 +383,25 @@
                 if df or ds:
                     yield lax.rem(my_f + df, nf), lax.rem(my_s + ds, ns)
 
-    for d in range(1, n):
-        t = lax.rem(me + d, n)
-        num_send[t] = numerator(t)
-        num_copy(t, me).start()
-    num_all[me, my_f, my_s] = numerator(me)
-    for f, s in siblings():
-        sib_copy(me, f, s, my_f, my_s).start()
+    def attend():
+        gather_heads()
+        for d in range(1, n):
+            t = lax.rem(me + d, n)
+            num_send[t] = numerator(t)
+            num_copy(t, me).start()
+        num_all[me, my_f, my_s] = numerator(me)
+        for f, s in siblings():
+            sib_copy(me, f, s, my_f, my_s).start()
+
+    def spread():
+        for d in range(1, n):
+            o = lax.rem(me + d, n)
+            num_copy(o, o).wait_recv()
+            for f, s in siblings():
+                sib_copy(o, f, s, my_f, my_s).start()
 
     for r in range(2, n):
-        o_stream.relay(r)
-        if r == 2:
-            for d in range(1, n):
-                o = lax.rem(me + d, n)
-                num_copy(o, o).wait_recv()
-                for f, s in siblings():
-                    sib_copy(o, f, s, my_f, my_s).start()
+        o_stream.relay(r, {2: attend, 3: spread}.get(r))
 
     for d in range(n):
         o = lax.rem(me + d, n)
@@ -344,8 +414,8 @@
         for s in range(ns):
             whole = jnp.concatenate([num_all[o, f, s] for f in range(nf)], 0).astype(F32)
             meansq = jnp.sum(whole * whole, axis=0, keepdims=True) / head_width
-            scaled = whole * lax.rsqrt(meansq + 1e-06) * head_gain_ref[...]
-            attended[o, :, s * head_width : (s + 1) * head_width] = scaled.T.astype(BF16)
+            scaled = (whole * lax.rsqrt(meansq + 1e-06)).T * head_gain_ref[...]
+            attended[o, :, s * head_width : (s + 1) * head_width] = scaled.astype(BF16)
         return carry
 
     lax.fori_loop(0, n, attend_block, 0)
@@ -385,8 +455,10 @@
 
 def per_device(sizes, tokens, norm_gain, w_query, w_key, w_value, head_gain, w_out):
     n, nf, ns = sizes
-    stacked = jnp.concatenate([w_query[0], w_key[0], w_value[0]], 0)
-    rows, width = stacked.shape
+    shards = [w_query[0], w_key[0], w_value[0]]
+    if any(shard.shape[0] % 8 for shard in shards):
+        shards = [jnp.concatenate(shards, 0)]
+    rows, width = sum(shard.shape[0] for shard in shards), tokens.shape[1]
     count = tokens.shape[0]
     qk_rows = w_query.shape[1] + w_key.shape[1]
     channels = w_value.shape[1]
@@ -394,14 +466,19 @@
     pieces = max(1, 16 // n)
     out_pieces = max(1, 16 // n)
     wo = w_out.reshape(ns, out_pieces, head_width // out_pieces, columns)
+    hbm = pl.BlockSpec(memory_space=pl.ANY)
     vmem = pl.BlockSpec(memory_space=pltpu.VMEM)
     dma = pltpu.SemaphoreType.DMA
     return pl.pallas_call(
-        functools.partial(kernel, n, nf, ns, pieces, out_pieces),
+        functools.partial(kernel, n, nf, ns, pieces, out_pieces, len(shards)),
         out_shape=jax.ShapeDtypeStruct((count, columns), BF16),
-        in_specs=[vmem] * 5,
+        in_specs=[hbm, vmem, vmem, hbm] + [hbm] * len(shards),
         out_specs=vmem,
         scratch_shapes=[
+            pltpu.VMEM(tokens.shape, BF16),
+            pltpu.VMEM((rows, width), BF16),
+            pltpu.VMEM(wo.shape, BF16),
+            dma((len(shards) + 2,)),
             pltpu.VMEM((2 * pieces, count, width // (2 * pieces)), BF16),
             pltpu.VMEM((n, 2, pieces, rows, width // (2 * pieces)), BF16),
             pltpu.VMEM((n,) + wo.shape, BF16),
@@ -429,9 +506,9 @@
             dma((n, nf, ns)),
         ],
         compiler_params=pltpu.CompilerParams(
-            has_side_effects=True, vmem_limit_bytes=60 * 1024 * 1024
+            collective_id=0, has_side_effects=True, vmem_limit_bytes=60 * 1024 * 1024
         ),
-    )(tokens, norm_gain.reshape(1, -1), stacked, head_gain.reshape(-1, 1), wo)
+    )(tokens, norm_gain.reshape(1, -1), head_gain.reshape(1, -1), wo, *shards)
 
 
 def solution(mesh):

time: 116 us -> 100 us (0.86)
  Pallas kernels: 109 us -> 97.5 us
  other arithmetic: 2.45 us -> 0 us
  local copies, waits for them, and re-layouts: 3.69 us -> 2.3 us
    pallas_call x1, Pallas kernels: 109 us -> 97.5 us  [per_device(): pl.pallas_call(functools.partial(kernel, n, nf, ns, pieces, out_pieces, l...]
    concatenate x1 -> x0, other arithmetic: 2.45 us -> none  [per_device(): stacked = jnp.concatenate([w_query[0], w_key[0], w_value[0]], 0)]
    reshape x1 -> x0, local copies, waits for them, and re-layouts: 1.39 us -> none  [per_device(): head_gain.reshape(-1, 1)]
where the time goes in v2:
time: 100 us; the launch traced here: 99.8 us
  Pallas kernels  97.5 us (98%)
  local copies, waits for them, and re-layouts  2.3 us (2%)
    pallas_call x1, Pallas kernels, per_device(): pl.pallas_call(functools.partial(kernel, n, nf, ns, pieces, out_pieces, l...  97.5 us
    unnamed x1, local copies, waits for them, and re-layouts  2.3 us

profile of v2, /device:TPU:0, one launch (start us, length us, event | category | flops | bytes accessed | tf_op | source)
XLA Modules:
  0.0 99.8 jit_solution(701053971173290675)
XLA Ops:
  0.0 97.5 %shard_map.73 = bf16[256,2048]{1,0:T(8,128)(2,1)} custom-call(bf16[256,8192]{1,0:T(8,128)(2,1)} %tok_hbm.1, f32[1,8192]{1,0:T(1,128)} %bitcast.10, f32[1,128]{1,0:T(1,128)} %bitcast.11, bf16[2,4,32,2048]{3,2,1,0:T(8,128)(2,1)} %bitcast.6, bf16[8,8192]{1,0:T(8,128)(2,1)} %bitcast.8, bf16[8,8192]{1,0:T(8,128)(2,1)} %bitcast.9, bf16[64,8192]{1,0:T(8,128)(2,1)} %bitcast.7), custom_call_target="tpu_custom_call" | custom-call | tf_op jit(solution)/shard_map/pallas_call | solution.py:472
  97.5 2.3 %copy.9 = bf16[256,2048]{1,0:T(8,128)(2,1)} copy(bf16[256,2048]{1,0:T(8,128)(2,1)} %shard_map.73) | data formatting | bytes 2097152
